TPU v7x, 32 devices: a whole 2x2x4 slice. The times are simulated.
32 devices in a mesh: member: 2 (over y), blk: 16 (over z, x, core).
Axes of the slice: x: 2, y: 2, z: 4, core: 2. Of those that a mesh axis runs over, the one named last changes fastest.
Arguments:
- heat_anomaly: float32 [8, 1536, 512], P('member', 'blk'), parts along dimension 0, may hold values from -6 to 6
- saltiness_anomaly: float32 [8, 1536, 512], P('member', 'blk'), parts along dimension 0, may hold values from -6 to 6
- first_axis_flow: float32 [8, 1536, 512], P('member', 'blk'), parts along dimension 0, may hold values from -4 to 4
- second_axis_flow: float32 [8, 1536, 512], P('member', 'blk'), parts along dimension 0, may hold values from -4 to 4
- layer_spacing: float32 [4], replicated, may hold values from 0.5 to 4
- diagonal_shift: float32 [1536, 512], P('blk'), may hold values from 0.02 to 0.2
- water_tile_flags: int32 [16, 8], P('blk'), may hold values 0 or 1
Outputs:
- new_temperature: bfloat16 [8, 1536, 512], P('member', 'blk'), parts along dimension 0
- new_salinity: bfloat16 [8, 1536, 512], P('member', 'blk'), parts along dimension 0
- new_u: bfloat16 [8, 1536, 512], P('member', 'blk'), parts along dimension 0
- new_v: bfloat16 [8, 1536, 512], P('member', 'blk'), parts along dimension 0
- height: float32 [3072, 512], P(('member', 'blk')), parts along dimension 0
- residual: float32 [3072, 512], P(('member', 'blk')), parts along dimension 0
There are 2 independent parts, one for each index of `member`. A program takes and returns all parts, laid end to end along the dimension named above; an argument that names none is the same for every part. Nothing has to cross between parts.
Inputs may be any that keep to these rules, and one draw needn't show every extreme that they name: `water_tile_flags`: 1 marks an ocean block, 0 a land block.
All inputs are finite; a program needn't handle non-finite values.
Results may differ from a plain program's by a relative error of at most 0.001.
Values sent between devices are 32-bit elements; how exact they have to be, the bound alone decides.
A program may use at most 128 MiB of HBM per device.

v0:
```python
import functools

import jax
import jax.numpy as jnp
import numpy as np
from jax import lax
from jax.experimental import pallas as pl
from jax.experimental.pallas import tpu as pltpu
from jax.sharding import PartitionSpec as P

SSTEP = 4
CG_BLOCKS = 3
COURANT = 0.2
DEEP = 16
PAD = 8
STRIP = 16
NEAR = 8
F32 = jnp.float32
HIGHEST = lax.Precision.HIGHEST


def shift_table(powers):
    extent = 2 * powers + 1
    table = np.zeros((extent, extent), np.float32)
    for offset, count in ((0, powers), (powers + 1, powers - 1)):
        for place in range(count):
            source = offset + place
            if place == 0:
                table[source + 1, source] = 0.5
                table[source, source] = 0.5
            else:
                table[source + 1, source] = 0.25
                table[source, source] = 0.5
                table[source - 1, source] = 0.25
    return table


def quadratic(gram, left, right):
    total = None
    for i, li in enumerate(left):
        if li is None:
            continue
        row = None
        for j, rj in enumerate(right):
            if rj is None:
                continue
            term = gram[i][j] * rj
            row = term if row is None else row + term
        term = li * row
        total = term if total is None else total + term
    return total


def plus(a, b):
    if a is None:
        return b
    if b is None:
        return a
    return a + b


def scaled(scale, a):
    return None if a is None else scale * a


def inner_steps(gram, powers):
    extent = 2 * powers + 1
    table = shift_table(powers)
    one = jnp.ones_like(gram[0][0])
    along = [one if i == 0 else None for i in range(extent)]
    resid = [one if i == powers + 1 else None for i in range(extent)]
    offset = [None] * extent
    norm_now = quadratic(gram, resid, resid)
    for sweep in range(powers):
        image = []
        for i in range(extent):
            total = None
            for j in range(extent):
                if table[i, j] != 0.0:
                    total = plus(total, scaled(float(table[i, j]), along[j]))
            image.append(total)
        alpha = norm_now / quadratic(gram, along, image)
        offset = [plus(o, scaled(alpha, a)) for o, a in zip(offset, along)]
        resid = [plus(r, scaled(-alpha, a)) for r, a in zip(resid, image)]
        norm_next = quadratic(gram, resid, resid)
        beta = norm_next / norm_now
        along = [plus(r, scaled(beta, a)) for r, a in zip(resid, along)]
        norm_now = norm_next
    return offset, resid, along


def kernel(
    n,
    heat, salt, uvel, vvel, spacing, damp, flags,
    o_heat, o_salt, o_u, o_v, o_height, o_resid,
    ue, ve, he, se, de, oc, oce, a4, tu, tv, basis, hgt, res,
    bh, bs, bu, bv, pairs, slots,
    lsem, osem, hs_sem, hr_sem, gs_sem, gr_sem,
):
    levels, rows, lanes = uvel.shape
    base = PAD + DEEP
    total = rows + 2 * base
    me = lax.axis_index("blk")
    right, left = lax.rem(me + 1, n), lax.rem(me + n - 1, n)

    loads = [
        pltpu.make_async_copy(uvel, ue.at[:, pl.ds(base, rows)], lsem.at[0]),
        pltpu.make_async_copy(vvel, ve.at[:, pl.ds(base, rows)], lsem.at[1]),
        pltpu.make_async_copy(damp, de.at[pl.ds(base, rows)], lsem.at[2]),
        pltpu.make_async_copy(heat, he.at[:, pl.ds(NEAR, rows)], lsem.at[3]),
        pltpu.make_async_copy(salt, se.at[:, pl.ds(NEAR, rows)], lsem.at[4]),
    ]
    for load in loads:
        load.start()

    barrier = pltpu.get_barrier_semaphore()
    for k in range(1, n):
        pl.semaphore_signal(
            barrier, inc=1, device_id={"blk": lax.rem(me + k, n)},
            device_id_type=pl.DeviceIdType.MESH,
        )

    tiles = flags.shape[1]
    lane_tile = lax.broadcasted_iota(jnp.int32, (8, lanes), 1) // (lanes // tiles)
    own = jnp.zeros((8, lanes), F32)
    for k in range(tiles):
        own = jnp.where(lane_tile == k, flags[0, k].astype(F32), own)
    oc[1] = own
    for ref in (ue, ve):
        ref[:, 0:PAD] = jnp.zeros((levels, PAD, lanes), F32)
        ref[:, total - PAD : total] = jnp.zeros((levels, PAD, lanes), F32)
    for ref in (oce, tu):
        ref[0:PAD] = jnp.zeros((PAD, lanes), F32)
        ref[total - PAD : total] = jnp.zeros((PAD, lanes), F32)
    for k in range(2 * SSTEP + 1):
        basis[k, 0 : 2 * PAD] = jnp.zeros((2 * PAD, lanes), F32)
        basis[k, total - 2 * PAD : total] = jnp.zeros((2 * PAD, lanes), F32)
    pairs[...] = jnp.zeros_like(pairs)
    for r in range(base, base + rows, 8):
        oce[r : r + 8] = own

    pl.semaphore_wait(barrier, n - 1)

    sends = []

    def send(k, src, dst, to, way):
        copy = pltpu.make_async_remote_copy(
            src_ref=src, dst_ref=dst,
            send_sem=hs_sem.at[k, way], recv_sem=hr_sem.at[k, way],
            device_id={"blk": to}, device_id_type=pl.DeviceIdType.MESH,
        )
        copy.start()
        sends.append(copy)
        return copy

    halos = {}

    def exchange3(k, ref, start, depth):
        halos[k] = [
            send(k, ref.at[:, pl.ds(start + rows - depth, depth)],
                 ref.at[:, pl.ds(start - depth, depth)], right, 0),
            send(k, ref.at[:, pl.ds(start, depth)],
                 ref.at[:, pl.ds(start + rows, depth)], left, 1),
        ]

    halos[3] = [
        send(3, oc.at[1], oc.at[0], right, 0),
        send(3, oc.at[1], oc.at[2], left, 1),
    ]
    loads[0].wait()
    exchange3(0, ue, base, DEEP)
    loads[1].wait()
    exchange3(1, ve, base, DEEP)
    loads[2].wait()
    halos[2] = [
        send(2, de.at[pl.ds(base + rows - DEEP, DEEP)],
             de.at[pl.ds(base - DEEP, DEEP)], right, 0),
        send(2, de.at[pl.ds(base, DEEP)],
             de.at[pl.ds(base + rows, DEEP)], left, 1),
    ]
    loads[3].wait()
    exchange3(4, he, NEAR, NEAR)
    loads[4].wait()
    exchange3(5, se, NEAR, NEAR)

    lane = lax.broadcasted_iota(jnp.int32, (STRIP, lanes), 1)

    def north_of(x):
        return pltpu.roll(x, lanes - 1, 1)

    def south_of(x):
        return pltpu.roll(x, 1, 1)

    def faces(level, r):
        here = pl.ds(r, STRIP)
        u0, up, um = ue[level, here], ue[level, pl.ds(r + 1, STRIP)], ue[level, pl.ds(r - 1, STRIP)]
        v0 = ve[level, here]
        w0, wp, wm = oce[here], oce[pl.ds(r + 1, STRIP)], oce[pl.ds(r - 1, STRIP)]
        east = 0.5 * (u0 + up) * (w0 * wp)
        west = 0.5 * (um + u0) * (wm * w0)
        ahead = jnp.where(lane == lanes - 1, 0.0, w0 * north_of(w0))
        north = 0.5 * (v0 + north_of(v0)) * ahead
        return east, west, north, w0

    def advect(face, ref, level, r):
        east, west, north, w0 = face
        q0, qp, qm = ref[level, pl.ds(r, STRIP)], ref[level, pl.ds(r + 1, STRIP)], ref[level, pl.ds(r - 1, STRIP)]
        fe = east * jnp.where(east > 0.0, q0, qp)
        fw = west * jnp.where(west > 0.0, qm, q0)
        fn = north * jnp.where(north > 0.0, q0, north_of(q0))
        return w0 * (q0 - COURANT * ((fe - fw) + (fn - south_of(fn))))

    strips = list(range(PAD, total - PAD, STRIP))
    inner = [r for r in strips if r >= base + STRIP and r + STRIP < base + rows]
    outer = [r for r in strips if r not in inner]

    whole_w = jnp.zeros((8, 128), F32)
    for j in range(levels):
        whole_w = whole_w + spacing[j]
    portions = [(jnp.full((8, 128), spacing[j], F32) / whole_w)[0:1, 0:1] for j in range(levels)]

    def flows(which):
        for level in range(levels):
            for r in which:
                face = faces(level, r)
                for ref, acc, out in ((ue, tu, bu), (ve, tv, bv)):
                    new = advect(face, ref, level, r)
                    part = portions[level] * new
                    here = pl.ds(r, STRIP)
                    acc[here] = part if level == 0 else acc[here] + part
                    if base <= r < base + rows:
                        out[level, r - base : r - base + STRIP] = new.astype(jnp.bfloat16)

    flows(inner)

    for k in (3, 0, 1):
        for copy in halos[k]:
            copy.wait_recv()
    for r in range(PAD, base, 8):
        oce[r : r + 8] = oc[0]
    for r in range(base + rows, total - PAD, 8):
        oce[r : r + 8] = oc[2]

    flows(outer)
    stores = [
        pltpu.make_async_copy(bu, o_u, osem.at[0]),
        pltpu.make_async_copy(bv, o_v, osem.at[1]),
    ]
    for store in stores:
        store.start()

    for copy in halos[2]:
        copy.wait_recv()
    for r in strips:
        here = pl.ds(r, STRIP)
        w0 = oce[here]
        a4[here] = 0.5 * (w0 * (6.0 + de[here]) + (1.0 - w0)) - 2.0
        t0 = tv[here]
        north = jnp.where(lane == lanes - 1, 0.0, north_of(t0))
        south = jnp.where(lane == 0, 0.0, south_of(t0))
        east = tu[pl.ds(r + 1, STRIP)] - tu[pl.ds(r - 1, STRIP)]
        basis[0, here] = w0 * (0.5 * (east + (north - south)))

    def pieces(first, last):
        cuts, r = [], first
        while r < last:
            h = STRIP if r % STRIP == PAD % STRIP and r + STRIP <= last else 8
            cuts.append((r, h))
            r += h
        return cuts

    def chebyshev(cur, nxt, prev, first, last):
        for r, h in pieces(first, last):
            here = pl.ds(r, h)
            k0 = basis[cur, here]
            ku, kd = basis[cur, pl.ds(r - 1, h)], basis[cur, pl.ds(r + 1, h)]
            w0 = oce[here]
            if r in (base, base + rows) or r + h in (base, base + rows):
                ku = ku * oce[pl.ds(r - 1, h)]
                kd = kd * oce[pl.ds(r + 1, h)]
                vert = ku + kd
                z = w0 * k0 + 0.5 * vert
            else:
                vert = ku + kd
                z = w0 * (k0 + 0.5 * vert)
            ln = lane[0:h]
            side = jnp.where(ln == 0, 0.0, south_of(z)) + jnp.where(ln == lanes - 1, 0.0, north_of(z))
            half = a4[here] * k0 - (0.5 * w0) * (vert + side)
            basis[nxt, here] = 0.5 * half if prev is None else half - basis[prev, here]

    def gram_partial(count):
        pair_list = [(a, b) for a in range(count) for b in range(a, count)]

        def body(s, accs):
            r = pl.multiple_of(base + 8 * s, 8)
            accs = list(accs)
            for c in range(0, lanes, 128):
                vals = [basis[a, pl.ds(r, 8), c : c + 128] for a in range(count)]
                for i, (a, b) in enumerate(pair_list):
                    accs[i] = accs[i] + vals[a] * vals[b]
            return tuple(accs)

        accs = lax.fori_loop(
            0, rows // 8, body, tuple(jnp.zeros((8, 128), F32) for _ in pair_list)
        )
        for i, acc in enumerate(accs):
            pairs[i : i + 1, :] = jnp.sum(acc, axis=0, keepdims=True)
        ones = jnp.ones((8, 128), F32)
        sums = lax.dot_general(
            ones, pairs[...], (((1,), (1,)), ((), ())),
            precision=HIGHEST, preferred_element_type=F32,
        )
        return pair_list, sums[0:1]

    def gram_send(b, row):
        slots[b, me] = row
        copies = []
        for k in range(1, n):
            to = lax.rem(me + k, n)
            copy = pltpu.make_async_remote_copy(
                src_ref=slots.at[b, me], dst_ref=slots.at[b, me],
                send_sem=gs_sem.at[b, k], recv_sem=gr_sem.at[b, k],
                device_id={"blk": to}, device_id_type=pl.DeviceIdType.MESH,
            )
            copy.start()
            copies.append(copy)
        return copies

    def gram_take(b, copies, pair_list):
        for k in range(1, n):
            src = lax.rem(me + n - k, n)
            pltpu.make_async_remote_copy(
                src_ref=slots.at[b, src], dst_ref=slots.at[b, src],
                send_sem=gs_sem.at[b, k], recv_sem=gr_sem.at[b, k],
                device_id={"blk": src}, device_id_type=pl.DeviceIdType.MESH,
            ).wait_recv()
        row = slots[b, 0]
        for i in range(1, n):
            row = row + slots[b, i]
        row = jnp.broadcast_to(row, (8, 128))
        return {
            pair: jnp.broadcast_to(row[:, i : i + 1], (8, 128))
            for i, pair in enumerate(pair_list)
        }

    def tracers(chosen):
        for level in chosen:
            for r in range(0, rows, STRIP):
                face = faces(level, base + r)
                here = pl.ds(r, STRIP)
                bh[level, here] = advect(face, he, level, NEAR + r).astype(jnp.bfloat16)
                bs[level, here] = advect(face, se, level, NEAR + r).astype(jnp.bfloat16)

    shares = [list(range(levels))[i::CG_BLOCKS] for i in range(CG_BLOCKS)]
    group = SSTEP + 1
    for b in range(CG_BLOCKS):
        depth = DEEP if b == 0 else 8
        first, last = base - depth, base + rows + depth
        for p in range(SSTEP):
            chebyshev(p, p + 1, None if p == 0 else p - 1, first, last)
        if b > 0:
            for p in range(SSTEP - 1):
                q = group + p
                chebyshev(q, q + 1, None if p == 0 else q - 1, first, last)
        count = group if b == 0 else 2 * SSTEP + 1
        pair_list, row = gram_partial(count)
        copies = gram_send(b, row)
        if b == 0:
            for k in (4, 5):
                for copy in halos[k]:
                    copy.wait_recv()
        tracers(shares[b])
        if b == CG_BLOCKS - 1:
            for k, (buf, out) in enumerate(((bh, o_heat), (bs, o_salt))):
                store = pltpu.make_async_copy(buf, out, osem.at[2 + k])
                store.start()
                stores.append(store)
        got = gram_take(b, copies, pair_list)

        def place(i):
            return i - group if b == 0 and i >= group else i

        gram = [
            [got[tuple(sorted((place(i), place(j))))] for j in range(2 * SSTEP + 1)]
            for i in range(2 * SSTEP + 1)
        ]
        coefs = inner_steps(gram, SSTEP)
        merged = []
        for coef in coefs:
            out = [None] * count
            for i, c in enumerate(coef):
                out[place(i)] = plus(out[place(i)], c)
            merged.append(out)
        offset, resid, along = merged
        final = b == CG_BLOCKS - 1

        def combine(vals, coef):
            out = None
            for v, c in zip(vals, coef):
                if c is not None:
                    out = plus(out, c * v)
            return out

        def update(s, carry, own_rows):
            r = pl.multiple_of(s * 8, 8)
            for c in range(0, lanes, 128):
                here = (pl.ds(r, 8), slice(c, c + 128))
                vals = [basis[(i,) + here] for i in range(count)]
                if own_rows:
                    to = (pl.ds(pl.multiple_of(r - base, 8), 8), slice(c, c + 128))
                    step = combine(vals, offset)
                    hgt[to] = step if b == 0 else hgt[to] + step
                if final:
                    res[to] = combine(vals, resid)
                else:
                    basis[(group,) + here] = combine(vals, resid)
                    basis[(0,) + here] = combine(vals, along)
            return carry

        if not final:
            for r in (base - 8, base + rows):
                update(r // 8, 0, False)
        lax.fori_loop(base // 8, (base + rows) // 8, lambda s, c: update(s, c, True), 0)
        for copy in copies:
            copy.wait_send()

    for k, (buf, out) in enumerate(((hgt, o_height), (res, o_resid))):
        store = pltpu.make_async_copy(buf, out, osem.at[4 + k])
        store.start()
        stores.append(store)
    for copy in sends:
        copy.wait_send()
    for store in stores:
        store.wait()


def on_device(heat, salt, uvel, vvel, spacing, damp, flags):
    n = lax.axis_size("blk")
    levels, rows, lanes = uvel.shape
    total = rows + 2 * (PAD + DEEP)
    near = rows + 2 * NEAR
    hbm = pl.BlockSpec(memory_space=pl.ANY)
    smem = pl.BlockSpec(memory_space=pltpu.SMEM)
    half = jax.ShapeDtypeStruct((levels, rows, lanes), jnp.bfloat16)
    flat = jax.ShapeDtypeStruct((rows, lanes), F32)
    vm = pltpu.VMEM
    return pl.pallas_call(
        functools.partial(kernel, n),
        out_shape=(half, half, half, half, flat, flat),
        in_specs=[hbm, hbm, hbm, hbm, smem, hbm, smem],
        out_specs=(hbm,) * 6,
        scratch_shapes=[
            vm((levels, total, lanes), F32),
            vm((levels, total, lanes), F32),
            vm((levels, near, lanes), F32),
            vm((levels, near, lanes), F32),
            vm((total, lanes), F32),
            vm((3, 8, lanes), F32),
            vm((total, lanes), F32),
            vm((total, lanes), F32),
            vm((total, lanes), F32),
            vm((total, lanes), F32),
            vm((2 * SSTEP + 1, total, lanes), F32),
            vm((rows, lanes), F32),
            vm((rows, lanes), F32),
            vm((levels, rows, lanes), jnp.bfloat16),
            vm((levels, rows, lanes), jnp.bfloat16),
            vm((levels, rows, lanes), jnp.bfloat16),
            vm((levels, rows, lanes), jnp.bfloat16),
            vm((128, 128), F32),
            vm((CG_BLOCKS, n, 1, 128), F32),
            pltpu.SemaphoreType.DMA((5,)),
            pltpu.SemaphoreType.DMA((6,)),
            pltpu.SemaphoreType.DMA((6, 2)),
            pltpu.SemaphoreType.DMA((6, 2)),
            pltpu.SemaphoreType.DMA((CG_BLOCKS, n)),
            pltpu.SemaphoreType.DMA((CG_BLOCKS, n)),
        ],
        compiler_params=pltpu.CompilerParams(
            collective_id=0, has_side_effects=True, vmem_limit_bytes=48 * 1024 * 1024
        ),
    )(heat, salt, uvel, vvel, spacing, damp, flags)


def solution(mesh):
    return jax.shard_map(
        on_device,
        mesh=mesh,
        in_specs=(
            P("member", "blk", None),
            P("member", "blk", None),
            P("member", "blk", None),
            P("member", "blk", None),
            P(),
            P("blk", None),
            P("blk", None),
        ),
        out_specs=(
            P("member", "blk", None),
            P("member", "blk", None),
            P("member", "blk", None),
            P("member", "blk", None),
            P(("member", "blk"), None),
            P(("member", "blk"), None),
        ),
        check_vma=False,
    )
```

profile of v0, /device:TPU:1, one launch (start us, length us, event | category | flops | bytes accessed | tf_op | source)
XLA Modules:
  0.0 51.6 jit_solution(7644722747611264057)
XLA Ops:
  0.6 0.0 copy-start
  0.6 1.1 %copy-done = f32[4,96,512]{2,1,0:T(8,128)S(1)} copy-done((f32[4,96,512]{2,1,0:T(8,128)S(1)}, f32[4,96,512]{2,1,0:T(8,128)}, u32[]{:S(2)}) %copy-start) | copy-done | bytes 786456
  1.8 0.0 copy-start.1
  1.8 1.1 %copy-done.1 = f32[4,96,512]{2,1,0:T(8,128)S(1)} copy-done((f32[4,96,512]{2,1,0:T(8,128)S(1)}, f32[4,96,512]{2,1,0:T(8,128)}, u32[]{:S(2)}) %copy-start.1) | copy-done | bytes 786456
  2.9 0.0 copy-start.2
  2.9 1.1 %copy-done.2 = f32[4,96,512]{2,1,0:T(8,128)S(1)} copy-done((f32[4,96,512]{2,1,0:T(8,128)S(1)}, f32[4,96,512]{2,1,0:T(8,128)}, u32[]{:S(2)}) %copy-start.2) | copy-done | bytes 786456
  4.0 0.0 copy-start.3
  4.0 1.1 %copy-done.3 = f32[4,96,512]{2,1,0:T(8,128)S(1)} copy-done((f32[4,96,512]{2,1,0:T(8,128)S(1)}, f32[4,96,512]{2,1,0:T(8,128)}, u32[]{:S(2)}) %copy-start.3) | copy-done | bytes 786456
  5.2 0.0 copy-start.4
  5.2 0.9 %copy-done.4 = f32[96,512]{1,0:T(8,128)S(1)} copy-done((f32[96,512]{1,0:T(8,128)S(1)}, f32[96,512]{1,0:T(8,128)}, u32[]{:S(2)}) %copy-start.4) | copy-done | bytes 196632
  6.1 0.0 copy-start.5
  6.1 0.7 %copy-done.5 = f32[4]{0:T(128)S(1)} copy-done((f32[4]{0:T(128)S(1)}, f32[4]{0:T(128)}, u32[]{:S(2)}) %copy-start.5) | copy-done | bytes 40
  6.8 0.0 copy-start.6
  6.8 0.7 %copy-done.6 = s32[1,8]{1,0:T(1,128)S(1)} copy-done((s32[1,8]{1,0:T(1,128)S(1)}, s32[1,8]{1,0:T(1,128)}, u32[]{:S(2)}) %copy-start.6) | copy-done | bytes 56
  7.4 39.9 %shard_map.118 = (bf16[4,96,512]{2,1,0:T(8,128)(2,1)S(1)}, bf16[4,96,512]{2,1,0:T(8,128)(2,1)S(1)}, bf16[4,96,512]{2,1,0:T(8,128)(2,1)S(1)}, bf16[4,96,512]{2,1,...) custom-call(f32[4,96,512]{2,1,0:T(8,128)S(1)} %copy-done, f32[4,96,512]{2,1,0:T(8,128)S(1)} %copy-done.1, ...), custom_call_target="tpu_custom_call" | custom-call | tf_op jit(solution)/shard_map/pallas_call | solution.py:447
  47.3 0.7 %copy.19 = bf16[4,96,512]{2,1,0:T(8,128)(2,1)} copy(bf16[4,96,512]{2,1,0:T(8,128)(2,1)S(1)} %get-tuple-element.12) | data formatting | bytes 786432
  48.1 0.7 %copy.20 = bf16[4,96,512]{2,1,0:T(8,128)(2,1)} copy(bf16[4,96,512]{2,1,0:T(8,128)(2,1)S(1)} %get-tuple-element.13) | data formatting | bytes 786432
  48.8 0.7 %copy.21 = bf16[4,96,512]{2,1,0:T(8,128)(2,1)} copy(bf16[4,96,512]{2,1,0:T(8,128)(2,1)S(1)} %get-tuple-element.14) | data formatting | bytes 786432
  49.5 0.7 %copy.22 = bf16[4,96,512]{2,1,0:T(8,128)(2,1)} copy(bf16[4,96,512]{2,1,0:T(8,128)(2,1)S(1)} %get-tuple-element.15) | data formatting | bytes 786432
  50.3 0.7 %copy.23 = f32[96,512]{1,0:T(8,128)} copy(f32[96,512]{1,0:T(8,128)S(1)} %get-tuple-element.16) | data formatting | bytes 393216
  51.0 0.7 %copy.24 = f32[96,512]{1,0:T(8,128)} copy(f32[96,512]{1,0:T(8,128)S(1)} %get-tuple-element.17) | data formatting | bytes 393216
Async XLA Ops:
  0.6 1.1 %copy-start = (f32[4,96,512]{2,1,0:T(8,128)S(1)}, f32[4,96,512]{2,1,0:T(8,128)}, u32[]{:S(2)}) copy-start(f32[4,96,512]{2,1,0:T(8,128)} %heat.1) | copy-start | bytes 2359300
  1.8 1.1 %copy-start.1 = (f32[4,96,512]{2,1,0:T(8,128)S(1)}, f32[4,96,512]{2,1,0:T(8,128)}, u32[]{:S(2)}) copy-start(f32[4,96,512]{2,1,0:T(8,128)} %salt.1) | copy-start | bytes 2359300
  2.9 1.1 %copy-start.2 = (f32[4,96,512]{2,1,0:T(8,128)S(1)}, f32[4,96,512]{2,1,0:T(8,128)}, u32[]{:S(2)}) copy-start(f32[4,96,512]{2,1,0:T(8,128)} %uvel.1) | copy-start | bytes 2359300
  4.0 1.1 %copy-start.3 = (f32[4,96,512]{2,1,0:T(8,128)S(1)}, f32[4,96,512]{2,1,0:T(8,128)}, u32[]{:S(2)}) copy-start(f32[4,96,512]{2,1,0:T(8,128)} %vvel.1) | copy-start | bytes 2359300
  5.2 0.9 %copy-start.4 = (f32[96,512]{1,0:T(8,128)S(1)}, f32[96,512]{1,0:T(8,128)}, u32[]{:S(2)}) copy-start(f32[96,512]{1,0:T(8,128)} %damp.1) | copy-start | bytes 589828
  6.1 0.7 %copy-start.5 = (f32[4]{0:T(128)S(1)}, f32[4]{0:T(128)}, u32[]{:S(2)}) copy-start(f32[4]{0:T(128)} %spacing.1) | copy-start | bytes 52
  6.8 0.7 %copy-start.6 = (s32[1,8]{1,0:T(1,128)S(1)}, s32[1,8]{1,0:T(1,128)}, u32[]{:S(2)}) copy-start(s32[1,8]{1,0:T(1,128)} %flags.1) | copy-start | bytes 100
where the time goes:
time: 52.6 us; the launch traced here: 51.6 us
  Pallas kernels  39.9 us (76%)
  local copies, waits for them, and re-layouts  11.1 us (21%)
  between operations  0.66 us (1%)
    pallas_call x1, Pallas kernels, on_device(): pl.pallas_call(functools.partial(kernel, n), out_shape=(half, half, half,...  39.9 us
    unnamed x20, local copies, waits for them, and re-layouts  11.1 us

commit v1 on v0

--- a/solution.py
+++ b/solution.py
@@ -10,6 +10,8 @@
 
 SSTEP = 4
 CG_BLOCKS = 3
+SWEEPS = SSTEP * CG_BLOCKS
+FIELDS = SWEEPS + 1
 COURANT = 0.2
 DEEP = 16
 PAD = 8
@@ -19,36 +21,33 @@
 HIGHEST = lax.Precision.HIGHEST
 
 
-def shift_table(powers):
-    extent = 2 * powers + 1
+def shift_table(extent):
     table = np.zeros((extent, extent), np.float32)
-    for offset, count in ((0, powers), (powers + 1, powers - 1)):
-        for place in range(count):
-            source = offset + place
-            if place == 0:
-                table[source + 1, source] = 0.5
-                table[source, source] = 0.5
-            else:
-                table[source + 1, source] = 0.25
-                table[source, source] = 0.5
-                table[source - 1, source] = 0.25
+    for source in range(extent - 1):
+        if source == 0:
+            table[1, 0] = table[0, 0] = 0.5
+        else:
+            table[source + 1, source] = 0.25
+            table[source, source] = 0.5
+            table[source - 1, source] = 0.25
     return table
 
 
+def tree(terms):
+    while len(terms) > 1:
+        terms = [
+            terms[i] + terms[i + 1] if i + 1 < len(terms) else terms[i]
+            for i in range(0, len(terms), 2)
+        ]
+    return terms[0]
+
+
 def quadratic(gram, left, right):
-    total = None
+    rows = []
     for i, li in enumerate(left):
-        if li is None:
-            continue
-        row = None
-        for j, rj in enumerate(right):
-            if rj is None:
-                continue
-            term = gram[i][j] * rj
-            row = term if row is None else row + term
-        term = li * row
-        total = term if total is None else total + term
-    return total
+        if li is not None:
+            rows.append(li * tree([gram[i][j] * rj for j, rj in enumerate(right) if rj is not None]))
+    return tree(rows)
 
 
 def plus(a, b):
@@ -63,15 +62,15 @@
     return None if a is None else scale * a
 
 
-def inner_steps(gram, powers):
-    extent = 2 * powers + 1
-    table = shift_table(powers)
+def inner_steps(gram, sweeps):
+    extent = sweeps + 1
+    table = shift_table(extent)
     one = jnp.ones_like(gram[0][0])
-    along = [one if i == 0 else None for i in range(extent)]
-    resid = [one if i == powers + 1 else None for i in range(extent)]
+    along = [one] + [None] * sweeps
+    resid = [one] + [None] * sweeps
     offset = [None] * extent
     norm_now = quadratic(gram, resid, resid)
-    for sweep in range(powers):
+    for sweep in range(sweeps):
         image = []
         for i in range(extent):
             total = None
@@ -82,11 +81,12 @@
         alpha = norm_now / quadratic(gram, along, image)
         offset = [plus(o, scaled(alpha, a)) for o, a in zip(offset, along)]
         resid = [plus(r, scaled(-alpha, a)) for r, a in zip(resid, image)]
-        norm_next = quadratic(gram, resid, resid)
-        beta = norm_next / norm_now
-        along = [plus(r, scaled(beta, a)) for r, a in zip(resid, along)]
-        norm_now = norm_next
-    return offset, resid, along
+        if sweep + 1 < sweeps:
+            norm_next = quadratic(gram, resid, resid)
+            beta = norm_next / norm_now
+            along = [plus(r, scaled(beta, a)) for r, a in zip(resid, along)]
+            norm_now = norm_next
+    return offset, resid
 
 
 def kernel(
@@ -132,7 +132,7 @@
     for ref in (oce, tu):
         ref[0:PAD] = jnp.zeros((PAD, lanes), F32)
         ref[total - PAD : total] = jnp.zeros((PAD, lanes), F32)
-    for k in range(2 * SSTEP + 1):
+    for k in range(FIELDS):
         basis[k, 0 : 2 * PAD] = jnp.zeros((2 * PAD, lanes), F32)
         basis[k, total - 2 * PAD : total] = jnp.zeros((2 * PAD, lanes), F32)
     pairs[...] = jnp.zeros_like(pairs)
@@ -288,60 +288,23 @@
             half = a4[here] * k0 - (0.5 * w0) * (vert + side)
             basis[nxt, here] = 0.5 * half if prev is None else half - basis[prev, here]
 
-    def gram_partial(count):
-        pair_list = [(a, b) for a in range(count) for b in range(a, count)]
-
+    pair_list = [(a, b) for a in range(FIELDS) for b in range(a, FIELDS)]
+
+    def gram_partial(first, chosen):
         def body(s, accs):
             r = pl.multiple_of(base + 8 * s, 8)
             accs = list(accs)
             for c in range(0, lanes, 128):
-                vals = [basis[a, pl.ds(r, 8), c : c + 128] for a in range(count)]
-                for i, (a, b) in enumerate(pair_list):
+                vals = [basis[a, pl.ds(r, 8), c : c + 128] for a in range(FIELDS)]
+                for i, (a, b) in enumerate(chosen):
                     accs[i] = accs[i] + vals[a] * vals[b]
             return tuple(accs)
 
         accs = lax.fori_loop(
-            0, rows // 8, body, tuple(jnp.zeros((8, 128), F32) for _ in pair_list)
+            0, rows // 8, body, tuple(jnp.zeros((8, 128), F32) for _ in chosen)
         )
         for i, acc in enumerate(accs):
-            pairs[i : i + 1, :] = jnp.sum(acc, axis=0, keepdims=True)
-        ones = jnp.ones((8, 128), F32)
-        sums = lax.dot_general(
-            ones, pairs[...], (((1,), (1,)), ((), ())),
-            precision=HIGHEST, preferred_element_type=F32,
-        )
-        return pair_list, sums[0:1]
-
-    def gram_send(b, row):
-        slots[b, me] = row
-        copies = []
-        for k in range(1, n):
-            to = lax.rem(me + k, n)
-            copy = pltpu.make_async_remote_copy(
-                src_ref=slots.at[b, me], dst_ref=slots.at[b, me],
-                send_sem=gs_sem.at[b, k], recv_sem=gr_sem.at[b, k],
-                device_id={"blk": to}, device_id_type=pl.DeviceIdType.MESH,
-            )
-            copy.start()
-            copies.append(copy)
-        return copies
-
-    def gram_take(b, copies, pair_list):
-        for k in range(1, n):
-            src = lax.rem(me + n - k, n)
-            pltpu.make_async_remote_copy(
-                src_ref=slots.at[b, src], dst_ref=slots.at[b, src],
-                send_sem=gs_sem.at[b, k], recv_sem=gr_sem.at[b, k],
-                device_id={"blk": src}, device_id_type=pl.DeviceIdType.MESH,
-            ).wait_recv()
-        row = slots[b, 0]
-        for i in range(1, n):
-            row = row + slots[b, i]
-        row = jnp.broadcast_to(row, (8, 128))
-        return {
-            pair: jnp.broadcast_to(row[:, i : i + 1], (8, 128))
-            for i, pair in enumerate(pair_list)
-        }
+            pairs[first + i : first + i + 1, :] = jnp.sum(acc, axis=0, keepdims=True)
 
     def tracers(chosen):
         for level in chosen:
@@ -351,78 +314,63 @@
                 bh[level, here] = advect(face, he, level, NEAR + r).astype(jnp.bfloat16)
                 bs[level, here] = advect(face, se, level, NEAR + r).astype(jnp.bfloat16)
 
-    shares = [list(range(levels))[i::CG_BLOCKS] for i in range(CG_BLOCKS)]
-    group = SSTEP + 1
-    for b in range(CG_BLOCKS):
-        depth = DEEP if b == 0 else 8
-        first, last = base - depth, base + rows + depth
-        for p in range(SSTEP):
-            chebyshev(p, p + 1, None if p == 0 else p - 1, first, last)
-        if b > 0:
-            for p in range(SSTEP - 1):
-                q = group + p
-                chebyshev(q, q + 1, None if p == 0 else q - 1, first, last)
-        count = group if b == 0 else 2 * SSTEP + 1
-        pair_list, row = gram_partial(count)
-        copies = gram_send(b, row)
-        if b == 0:
-            for k in (4, 5):
-                for copy in halos[k]:
-                    copy.wait_recv()
-        tracers(shares[b])
-        if b == CG_BLOCKS - 1:
-            for k, (buf, out) in enumerate(((bh, o_heat), (bs, o_salt))):
-                store = pltpu.make_async_copy(buf, out, osem.at[2 + k])
-                store.start()
-                stores.append(store)
-        got = gram_take(b, copies, pair_list)
-
-        def place(i):
-            return i - group if b == 0 and i >= group else i
-
-        gram = [
-            [got[tuple(sorted((place(i), place(j))))] for j in range(2 * SSTEP + 1)]
-            for i in range(2 * SSTEP + 1)
-        ]
-        coefs = inner_steps(gram, SSTEP)
-        merged = []
-        for coef in coefs:
-            out = [None] * count
-            for i, c in enumerate(coef):
-                out[place(i)] = plus(out[place(i)], c)
-            merged.append(out)
-        offset, resid, along = merged
-        final = b == CG_BLOCKS - 1
-
-        def combine(vals, coef):
-            out = None
-            for v, c in zip(vals, coef):
-                if c is not None:
-                    out = plus(out, c * v)
-            return out
-
-        def update(s, carry, own_rows):
-            r = pl.multiple_of(s * 8, 8)
-            for c in range(0, lanes, 128):
-                here = (pl.ds(r, 8), slice(c, c + 128))
-                vals = [basis[(i,) + here] for i in range(count)]
-                if own_rows:
-                    to = (pl.ds(pl.multiple_of(r - base, 8), 8), slice(c, c + 128))
-                    step = combine(vals, offset)
-                    hgt[to] = step if b == 0 else hgt[to] + step
-                if final:
-                    res[to] = combine(vals, resid)
-                else:
-                    basis[(group,) + here] = combine(vals, resid)
-                    basis[(0,) + here] = combine(vals, along)
-            return carry
-
-        if not final:
-            for r in (base - 8, base + rows):
-                update(r // 8, 0, False)
-        lax.fori_loop(base // 8, (base + rows) // 8, lambda s, c: update(s, c, True), 0)
-        for copy in copies:
-            copy.wait_send()
+    for p in range(SWEEPS):
+        reach = -(-(SWEEPS - p - 1) // 8) * 8
+        chebyshev(p, p + 1, None if p == 0 else p - 1, base - reach, base + rows + reach)
+    half = (len(pair_list) + 1) // 2
+    gram_partial(0, pair_list[:half])
+    gram_partial(half, pair_list[half:])
+    sums = lax.dot_general(
+        jnp.ones((8, 128), F32), pairs[...], (((1,), (1,)), ((), ())),
+        precision=HIGHEST, preferred_element_type=F32,
+    )
+    slots[me] = sums[0:1]
+    copies = []
+    for k in range(1, n):
+        copy = pltpu.make_async_remote_copy(
+            src_ref=slots.at[me], dst_ref=slots.at[me],
+            send_sem=gs_sem.at[k], recv_sem=gr_sem.at[k],
+            device_id={"blk": lax.rem(me + k, n)}, device_id_type=pl.DeviceIdType.MESH,
+        )
+        copy.start()
+        copies.append(copy)
+
+    for k in (4, 5):
+        for copy in halos[k]:
+            copy.wait_recv()
+    tracers(range(levels))
+    for k, (buf, out) in enumerate(((bh, o_heat), (bs, o_salt))):
+        store = pltpu.make_async_copy(buf, out, osem.at[2 + k])
+        store.start()
+        stores.append(store)
+
+    for k in range(1, n):
+        src = lax.rem(me + n - k, n)
+        pltpu.make_async_remote_copy(
+            src_ref=slots.at[src], dst_ref=slots.at[src],
+            send_sem=gs_sem.at[k], recv_sem=gr_sem.at[k],
+            device_id={"blk": src}, device_id_type=pl.DeviceIdType.MESH,
+        ).wait_recv()
+    row = jnp.broadcast_to(tree([slots[i] for i in range(n)]), (8, 128))
+    gram = [[None] * FIELDS for _ in range(FIELDS)]
+    for i, (a, b) in enumerate(pair_list):
+        gram[a][b] = gram[b][a] = jnp.broadcast_to(row[:, i : i + 1], (8, 128))
+    offset, resid = inner_steps(gram, SWEEPS)
+
+    def combine(vals, coef):
+        return tree([c * v for v, c in zip(vals, coef) if c is not None])
+
+    def update(s, carry):
+        r = pl.multiple_of(s * 8, 8)
+        for c in range(0, lanes, 128):
+            vals = [basis[i, pl.ds(pl.multiple_of(base + r, 8), 8), c : c + 128] for i in range(FIELDS)]
+            hgt[pl.ds(r, 8), c : c + 128] = combine(vals, offset)
+            res[pl.ds(r, 8), c : c + 128] = combine(vals, resid)
+        return carry
+
+    lax.fori_loop(0, rows // 8, update, 0)
+    for copy in copies:
+        copy.wait_send()
 
     for k, (buf, out) in enumerate(((hgt, o_height), (res, o_resid))):
         store = pltpu.make_async_copy(buf, out, osem.at[4 + k])
@@ -434,21 +382,38 @@
         store.wait()
 
 
+def drain(*refs):
+    count = len(refs) // 2
+    sems = refs[-1]
+    copies = [
+        pltpu.make_async_copy(refs[i], refs[count + i], sems.at[i]) for i in range(count)
+    ]
+    for copy in copies:
+        copy.start()
+    for copy in copies:
+        copy.wait()
+
+
 def on_device(heat, salt, uvel, vvel, spacing, damp, flags):
     n = lax.axis_size("blk")
     levels, rows, lanes = uvel.shape
     total = rows + 2 * (PAD + DEEP)
     near = rows + 2 * NEAR
-    hbm = pl.BlockSpec(memory_space=pl.ANY)
+    hbm = pl.BlockSpec(memory_space=pltpu.HBM)
+    free = pl.BlockSpec(memory_space=pl.ANY)
     smem = pl.BlockSpec(memory_space=pltpu.SMEM)
+    heat, salt, uvel, vvel, damp = (
+        pltpu.with_memory_space_constraint(x, pltpu.HBM) for x in (heat, salt, uvel, vvel, damp)
+    )
     half = jax.ShapeDtypeStruct((levels, rows, lanes), jnp.bfloat16)
     flat = jax.ShapeDtypeStruct((rows, lanes), F32)
     vm = pltpu.VMEM
-    return pl.pallas_call(
+    shapes = (half, half, half, half, flat, flat)
+    results = pl.pallas_call(
         functools.partial(kernel, n),
-        out_shape=(half, half, half, half, flat, flat),
+        out_shape=shapes,
         in_specs=[hbm, hbm, hbm, hbm, smem, hbm, smem],
-        out_specs=(hbm,) * 6,
+        out_specs=(free,) * 6,
         scratch_shapes=[
             vm((levels, total, lanes), F32),
             vm((levels, total, lanes), F32),
@@ -460,7 +425,7 @@
             vm((total, lanes), F32),
             vm((total, lanes), F32),
             vm((total, lanes), F32),
-            vm((2 * SSTEP + 1, total, lanes), F32),
+            vm((FIELDS, total, lanes), F32),
             vm((rows, lanes), F32),
             vm((rows, lanes), F32),
             vm((levels, rows, lanes), jnp.bfloat16),
@@ -468,18 +433,26 @@
             vm((levels, rows, lanes), jnp.bfloat16),
             vm((levels, rows, lanes), jnp.bfloat16),
             vm((128, 128), F32),
-            vm((CG_BLOCKS, n, 1, 128), F32),
+            vm((n, 1, 128), F32),
             pltpu.SemaphoreType.DMA((5,)),
             pltpu.SemaphoreType.DMA((6,)),
             pltpu.SemaphoreType.DMA((6, 2)),
             pltpu.SemaphoreType.DMA((6, 2)),
-            pltpu.SemaphoreType.DMA((CG_BLOCKS, n)),
-            pltpu.SemaphoreType.DMA((CG_BLOCKS, n)),
+            pltpu.SemaphoreType.DMA((n,)),
+            pltpu.SemaphoreType.DMA((n,)),
         ],
         compiler_params=pltpu.CompilerParams(
             collective_id=0, has_side_effects=True, vmem_limit_bytes=48 * 1024 * 1024
         ),
     )(heat, salt, uvel, vvel, spacing, damp, flags)
+    results = [pltpu.with_memory_space_constraint(x, pltpu.VMEM) for x in results]
+    return pl.pallas_call(
+        drain,
+        out_shape=tuple(pltpu.HBM(x.shape, x.dtype) for x in shapes),
+        in_specs=[pl.BlockSpec(memory_space=pltpu.VMEM)] * 6,
+        out_specs=(hbm,) * 6,
+        scratch_shapes=[pltpu.SemaphoreType.DMA((6,))],
+    )(*results)
 
 
 def solution(mesh):

time: 52.6 us -> 33.1 us (0.63); the launches traced: 51.6 us -> 32.9 us
  local copies, waits for them, and re-layouts: 11.1 us -> 1.3 us
  Pallas kernels: 39.9 us -> 30.9 us
    unnamed x20 -> x4, local copies, waits for them, and re-layouts: 11.1 us -> 1.3 us
    pallas_call x1 -> x2, Pallas kernels: 39.9 us -> 30.9 us  [the longest x1 29.6 us: on_device(): pl.pallas_call(functools.partial(kernel, n), out_shape=shapes, in_specs=[...]
where the time goes in v1:
time: 33.1 us; the launch traced here: 32.9 us
  Pallas kernels  30.9 us (93%)
  local copies, waits for them, and re-layouts  1.3 us (4%)
  between operations  0.65 us (2%)
    pallas_call x1, Pallas kernels, on_device(): pl.pallas_call(functools.partial(kernel, n), out_shape=shapes, in_specs=[...  29.6 us
    pallas_call x1, Pallas kernels, on_device(): pl.pallas_call(drain, out_shape=tuple((pltpu.HBM(x.shape, x.dtype) for x...  1.31 us
    unnamed x4, local copies, waits for them, and re-layouts  1.3 us

profile of v1, /device:TPU:1, one launch (start us, length us, event | category | flops | bytes accessed | tf_op | source)
XLA Modules:
  0.0 32.9 jit_solution(14204700002389582109)
XLA Ops:
  0.6 0.0 copy-start
  0.6 0.6 %copy-done = f32[4]{0:T(128)S(1)} copy-done((f32[4]{0:T(128)S(1)}, f32[4]{0:T(128)}, u32[]{:S(2)}) %copy-start) | copy-done | bytes 40
  1.3 0.0 copy-start.1
  1.3 0.7 %copy-done.1 = s32[1,8]{1,0:T(1,128)S(1)} copy-done((s32[1,8]{1,0:T(1,128)S(1)}, s32[1,8]{1,0:T(1,128)}, u32[]{:S(2)}) %copy-start.1) | copy-done | bytes 56
  1.9 29.6 %shard_map.118 = (bf16[4,96,512]{2,1,0:T(8,128)(2,1)S(1)}, bf16[4,96,512]{2,1,0:T(8,128)(2,1)S(1)}, bf16[4,96,512]{2,1,0:T(8,128)(2,1)S(1)}, bf16[4,96,512]{2,1,...) custom-call(f32[4,96,512]{2,1,0:T(8,128)} %heat.1, f32[4,96,512]{2,1,0:T(8,128)} %salt.1, ...), custom_call_target="tpu_custom_call" | custom-call | tf_op jit(solution)/shard_map/pallas_call | solution.py:412
  31.6 1.3 %shard_map.119 = (bf16[4,96,512]{2,1,0:T(8,128)(2,1)}, bf16[4,96,512]{2,1,0:T(8,128)(2,1)}, bf16[4,96,512]{2,1,0:T(8,128)(2,1)}, bf16[4,96,512]{2,1,0:T(8,128)(2...) custom-call(bf16[4,96,512]{2,1,0:T(8,128)(2,1)S(1)} %get-tuple-element.12.refs_0_, ...), custom_call_target="tpu_custom_call" | custom-call | tf_op jit(solution)/shard_map/pallas_call | solution.py:449
Async XLA Ops:
  0.6 0.7 %copy-start = (f32[4]{0:T(128)S(1)}, f32[4]{0:T(128)}, u32[]{:S(2)}) copy-start(f32[4]{0:T(128)} %spacing.1) | copy-start | bytes 52
  1.3 0.7 %copy-start.1 = (s32[1,8]{1,0:T(1,128)S(1)}, s32[1,8]{1,0:T(1,128)}, u32[]{:S(2)}) copy-start(s32[1,8]{1,0:T(1,128)} %flags.1) | copy-start | bytes 100
